TPU v7x, 128 devices: a whole 4x4x4 slice. The times are simulated.
128 devices in a mesh: row: 8 (over y, core), col: 16 (over z, x).
Axes of the slice: x: 4, y: 4, z: 4, core: 2. Of those that a mesh axis runs over, the one named last changes fastest.
Arguments:
- factors: bfloat16 [128, 2, 512, 512], P(('row', 'col')), as said below
- target: int32 [256, 1], P(('row', 'col')), may hold values from 0 to 127; in each aligned block of 256 rows (0 to 255, 256 to 511, ...) at most 3 rows name the same one
Outputs:
- roots: float32 [128, 3, 512, 512], P(('row', 'col'))
Inputs may be any that keep to these rules, and one draw needn't show every extreme that they name: `factors`: every block is symmetric and positive definite. `target`: every device receives between 1 and 3 blocks; some device receives exactly 3.
All inputs are finite; a program needn't handle non-finite values.
Results may differ from a plain program's by a relative error of at most 0.0003.
Values may be sent and summed in bfloat16 or wider, within the bound.
A program may use at most 128 MiB of HBM per device.

v0:
```python
import functools

import jax
import jax.numpy as jnp
from jax import lax
from jax.sharding import Mesh
from jax.sharding import PartitionSpec as P

ITERS = 3
CAP = 3
ROW = ("row_0", "row_1")
COL = ("col_0", "col_1")
ROW_COL = ("row_0", "row_1", "col_0", "col_1")


HIGH = lax.Precision.HIGHEST


def filled_with(value, identity):
    return jnp.broadcast_to(jnp.asarray(identity, value.dtype), value.shape)


def prefix_by_axis(value, axes, combine, identity):
    before = start = filled_with(value, identity)
    so_far = value
    for axis in reversed(axes):
        peers, index = (lax.axis_size(axis), lax.axis_index(axis))
        pieces = lax.all_gather(so_far, axis)
        inside, so_far = (start, start)
        for k in range(peers):
            passed = k < index
            so_far = combine(so_far, pieces[k])
            inside = jnp.where(passed, so_far, inside)
        before = combine(inside, before)
    return before


def over_axes(value, axes):
    return functools.reduce(lax.psum, axes, value)


def as_sent(value):
    return jax.tree.map(lambda a: a.astype(jnp.bfloat16) if a.dtype == jnp.float32 else a, value)


def add_counts(earlier, later):
    return earlier + later


def bucket(blocks, labels, group_keys, places, groups, room):
    item_total = blocks.shape[0]
    block_width = blocks.shape[1]
    wanted = jnp.where(labels[:, 0] > 0, group_keys * room + places, -1)
    chooser = jnp.arange(groups * room, dtype=jnp.int32)[:, None] == wanted[None, :]
    placed = jnp.dot(
        chooser.astype(jnp.bfloat16),
        blocks.reshape(item_total, block_width * block_width),
        preferred_element_type=jnp.float32,
    )
    placed = placed.astype(jnp.bfloat16).reshape(groups * room, block_width, block_width)
    placed_labels = jnp.dot(chooser.astype(jnp.int32), labels)
    return (placed, placed_labels)


def shards(factors, target):
    row_count = lax.axis_size(ROW)
    col_count = lax.axis_size(COL)
    device_count = row_count * col_count
    hold_count = factors.shape[1]
    block_width = factors.shape[2]
    my_row = lax.axis_index(ROW)
    targets = target[:, 0]
    peer_ids = jnp.arange(device_count, dtype=jnp.int32)
    matches = (targets[:, None] == peer_ids[None, :]).astype(jnp.int32)
    offsets_in = prefix_by_axis(
        jnp.sum(matches, axis=0), ROW_COL, add_counts, jnp.zeros((device_count,), jnp.int32)
    )
    earlier = jnp.cumsum(matches, axis=0) - matches
    slot_index = jnp.sum((earlier + offsets_in[None, :]) * matches, axis=1)
    blocks = factors[0]
    local_rows = jnp.zeros_like(targets) + my_row
    labels = jnp.stack(
        [jnp.ones_like(targets), targets // col_count, targets % col_count, slot_index, local_rows],
        axis=1,
    )
    row_ids = jnp.arange(row_count, dtype=jnp.int32)
    local_sq = jnp.sum(jnp.square(blocks.astype(jnp.float32)))
    row_terms = jnp.where(row_ids == my_row, local_sq, 0.0)
    layer_totals = over_axes(row_terms, ROW_COL)
    hold_places = jnp.arange(hold_count, dtype=jnp.int32)
    moved, moved_labels = bucket(blocks, labels, labels[:, 2], hold_places, col_count, hold_count)
    moved, moved_labels = (
        lax.all_to_all(moved, COL, split_axis=0, concat_axis=0, tiled=True),
        lax.all_to_all(as_sent(moved_labels), COL, split_axis=0, concat_axis=0, tiled=True).astype(
            moved_labels.dtype
        ),
    )
    moved, moved_labels = bucket(
        moved, moved_labels, moved_labels[:, 1], moved_labels[:, 3], row_count, CAP
    )
    moved, moved_labels = (
        lax.all_to_all(moved, ROW, split_axis=0, concat_axis=0, tiled=True),
        lax.all_to_all(as_sent(moved_labels), ROW, split_axis=0, concat_axis=0, tiled=True).astype(
            moved_labels.dtype
        ),
    )
    landed = jnp.sum(
        moved.reshape(row_count, CAP, block_width, block_width).astype(jnp.float32), axis=0
    )
    tags = jnp.sum(moved_labels.reshape(row_count, CAP, 5), axis=0)
    valid = tags[:, 0] > 0
    row_match = tags[:, 4][:, None] == row_ids[None, :]
    slot_totals = jnp.sum(jnp.where(row_match, layer_totals[None, :], 0.0), axis=1)
    scale = jnp.where(
        valid, 2.0 * jnp.sqrt(slot_totals / (col_count * hold_count * block_width)), 1.0
    )
    identity = jnp.eye(block_width, dtype=jnp.float32)
    moment = landed / scale[:, None, None]
    root_iter = jnp.broadcast_to(identity, landed.shape)
    for repeat in range(ITERS):
        step_mat = 1.25 * identity[None] - 0.25 * moment
        square_mat = jnp.einsum("bij,bjk->bik", step_mat, step_mat, precision=HIGH)
        fourth_mat = jnp.einsum("bij,bjk->bik", square_mat, square_mat, precision=HIGH)
        moment = jnp.einsum("bij,bjk->bik", fourth_mat, moment, precision=HIGH)
        root_iter = jnp.einsum("bij,bjk->bik", root_iter, step_mat, precision=HIGH)
    result = root_iter * (scale ** (-0.25))[:, None, None]
    result = jnp.where(valid[:, None, None], result, 0.0)
    return result[None]


def solution(mesh):
    finer = Mesh(mesh.devices.reshape(4, 2, 4, 4), ("row_0", "row_1", "col_0", "col_1"))
    placed = (P(ROW_COL, None, None, None), P(ROW_COL, None))
    return jax.shard_map(
        shards, mesh=finer, in_specs=placed, out_specs=P(ROW_COL, None, None, None), check_vma=False
    )
```

profile of v0, /device:TPU:1, one launch (start us, length us, event | category | flops | bytes accessed | tf_op | source)
XLA Modules:
  0.0 596.9 jit_solution(8716734078208463419)
XLA Ops:
  0.0 0.7 fusion.34
  0.7 0.7 fusion.33
  1.5 0.7 copy.25
  2.2 0.7 fusion.42
  2.9 8.5 %all-gather.1 = s32[4,1,128]{2,1,0:T(1,128)S(1)} all-gather(s32[1,1,128]{2,1,0:T(1,128)S(1)} %bitcast.69), channel_id=2, replica_groups=mesh['row_0'=4,'row_1'=2,'col_0'=4,'col_1'=4] {'col_1'}, dimensions={0}, use_global_device_ids=true | all-gather | bytes 2560 | tf_op jit(solution)/shard_map/all_gather | solution.py:28
  11.4 9.0 %all-gather.2 = s32[4,1,128]{2,1,0:T(1,128)S(1)} all-gather(s32[1,1,128]{2,1,0:T(1,128)S(1)} %slice_add_fusion.8), channel_id=1, replica_groups=mesh['row_0'=4,'row_1'=2,'col_0'=4,'col_1'=4] {'col_0'}, dimensions={0}, use_global_device_ids=true | all-gather | bytes 2560 | tf_op jit(solution)/shard_map/all_gather | solution.py:28
  20.4 6.2 %all-gather.3 = s32[2,1,128]{2,1,0:T(1,128)S(1)} all-gather(s32[1,1,128]{2,1,0:T(1,128)S(1)} %slice_add_fusion.5), channel_id=1, replica_groups=mesh['row_0'=4,'row_1'=2,'col_0'=4,'col_1'=4] {'row_1'}, dimensions={0}, use_global_device_ids=true | all-gather | bytes 1536 | tf_op jit(solution)/shard_map/all_gather | solution.py:28
  26.5 7.9 %all-gather.4 = s32[4,1,128]{2,1,0:T(1,128)S(1)} all-gather(s32[1,1,128]{2,1,0:T(1,128)S(1)} %slice_add_fusion.4), channel_id=1, replica_groups=mesh['row_0'=4,'row_1'=2,'col_0'=4,'col_1'=4] {'row_0'}, dimensions={0}, use_global_device_ids=true | all-gather | bytes 2560 | tf_op jit(solution)/shard_map/all_gather | solution.py:28
  34.5 0.8 select_reduce_fusion.1
  35.4 0.1 copy.29
  35.5 0.1 stack.13
  35.6 0.7 fusion.24
  36.3 3.5 all-to-all-start
  39.8 2.3 copy.40
  42.2 8.0 %convolution_convert_fusion = bf16[32,262144]{1,0:T(8,128)(2,1)} fusion(bf16[2,262144]{1,0:T(2,128)(2,1)S(1)} %bitcast.63, s32[2]{0:T(128)S(1)} %fusion.42), kind=kOutput, calls=%fused_computation | convolution fusion | flops 41943104 | bytes 17825800 | tf_op jit(solution)/shard_map/dot_general | solution.py:55
  50.2 16.6 %copy.41 = bf16[4,8,512,512]{3,2,1,0:T(8,128)(2,1)} copy(bf16[4,8,512,512]{3,1,2,0:T(8,128)(2,1)} %bitcast.59) | data formatting | bytes 33554432
  66.8 0.0 all-to-all-done
  66.8 6.6 %all-to-all-start.2 = ((bf16[32,512,512]{2,1,0:T(8,128)(2,1)}), bf16[32,512,512]{2,1,0:T(8,128)(2,1)}, u32[]{:S(2)}, u32[]{:S(2)}) async-start(bf16[32,512,512]{2,1,0:T(8,128)(2,1)} %bitcast.60), calls=%async_computation.2 | async-start | bytes 33554432 | tf_op jit(solution)/shard_map/all_to_all | solution.py:93
  73.5 0.2 fusion.23
  73.7 0.2 fusion.25
  73.9 0.6 copy.32
  74.5 240.2 %all-to-all-done.2 = bf16[32,512,512]{2,1,0:T(8,128)(2,1)} async-done(((bf16[32,512,512]{2,1,0:T(8,128)(2,1)}), bf16[32,512,512]{2,1,0:T(8,128)(2,1)}, u32[]{:S(2)}, u32[]{:S(2)}) %all-to-all-start.2) | async-done | bytes 16777248 | tf_op jit(solution)/shard_map/all_to_all | solution.py:93
  314.7 7.2 %all-to-all-start.1 = ((s32[8,3,5]{2,1,0:T(4,128)}), s32[8,3,5]{2,1,0:T(4,128)S(1)}, u32[]{:S(2)}, u32[]{:S(2)}) async-start(s32[8,3,5]{2,1,0:T(4,128)} %copy.32), calls=%async_computation.1 | async-start | bytes 32768 | tf_op jit(solution)/shard_map/all_to_all | solution.py:103
  321.9 18.5 %copy.42 = bf16[4,8,512,512]{3,1,2,0:T(8,128)(2,1)} copy(bf16[4,8,512,512]{3,2,1,0:T(8,128)(2,1)} %bitcast.24) | data formatting | bytes 33554432
  340.4 13.7 %convolution_convert_fusion.1 = bf16[24,262144]{1,0:T(8,128)(2,1)} fusion(bf16[32,262144]{1,0:T(8,128)(2,1)} %bitcast.58, s32[32]{0:T(128)S(1)} %fusion.23), kind=kOutput, calls=%fused_computation.1 | convolution fusion | flops 408945408 | bytes 29360256 | tf_op jit(solution)/shard_map/dot_general | solution.py:55
  354.1 12.8 %copy.43 = bf16[3,8,512,512]{3,2,1,0:T(8,128)(2,1)} copy(bf16[3,8,512,512]{3,1,2,0:T(8,128)(2,1)} %bitcast.61) | data formatting | bytes 25165824
  366.9 0.0 all-to-all-done.1
  366.9 0.0 copy-start
  366.9 5.4 all-to-all-start.3
  372.3 0.0 copy-done
  372.3 1.1 multiply_reduce_fusion
  373.5 0.6 compare_select_fusion.2
  374.1 138.3 %psum.28 = f32[8]{0:T(128)S(1)} all-reduce(f32[8]{0:T(128)S(1)} %compare_select_fusion.2), channel_id=1, replica_groups=mesh['row_0'=4,'row_1'=2,'col_0'=4,'col_1'=4] {'row_0'}, use_global_device_ids=true, to_apply=%region_6.7 | all-reduce | flops 8 | bytes 64 | tf_op jit(solution)/shard_map/psum | solution.py:39
  512.5 3.8 psum.29
  516.3 9.7 %psum.30 = f32[8]{0:T(128)S(1)} all-reduce(f32[8]{0:T(128)S(1)} %psum.29), channel_id=1, replica_groups=mesh['row_0'=4,'row_1'=2,'col_0'=4,'col_1'=4] {'col_0'}, use_global_device_ids=true, to_apply=%region_8.9 | all-reduce | flops 8 | bytes 64 | tf_op jit(solution)/shard_map/psum | solution.py:39
  526.0 6.4 %psum.31 = f32[8]{0:T(128)S(1)} all-reduce(f32[8]{0:T(128)S(1)} %psum.30), channel_id=1, replica_groups=mesh['row_0'=4,'row_1'=2,'col_0'=4,'col_1'=4] {'col_1'}, use_global_device_ids=true, to_apply=%region_9.10 | all-reduce | flops 8 | bytes 64 | tf_op jit(solution)/shard_map/psum | solution.py:39
  532.3 0.1 fusion.20
  532.5 0.1 fusion.21
  532.6 0.2 slice_reduce_fusion
  532.8 0.1 fusion.32
  532.9 0.2 select_reduce_fusion
  533.1 0.0 all-to-all-done.3
  533.1 8.4 %convert_reduce_fusion = f32[3,512,512]{2,1,0:T(8,128)} fusion(bf16[8,3,512,512]{3,2,1,0:T(8,128)(2,1)} %bitcast.18), kind=kLoop, calls=%fused_computation.2 | loop fusion | flops 11796480 | bytes 15728640 | tf_op jit(solution)/shard_map/reduce_sum | solution.py:107
  541.5 8.8 %fusion.3 = f32[3,512,512]{2,1,0:T(8,128)S(1)} fusion(f32[512,512]{1,0:T(8,128)S(1)} %fusion.20, f32[3,512,512]{2,1,0:T(8,128)} %convert_reduce_fusion, f32[3]{0:T(128)S(1)} %get-tuple-element.6), kind=kOutput, calls=%fused_computation.9 | convolution fusion | flops 4834197504 | bytes 7340044 | tf_op jit(solution)/shard_map/bij,bjk->bik/dot_general | solution.py:122
  550.3 0.0 copy-start.1
  550.3 5.7 fusion.51
  556.0 0.0 copy-done.1
  556.0 5.5 fusion.50
  561.5 5.5 fusion.5
  567.1 5.7 fusion.52
  572.8 5.3 fusion.53
  578.1 5.8 fusion.4
  583.9 5.4 fusion.6
  589.3 7.1 %select_bitcast_fusion = f32[1,3,512,512]{3,2,1,0:T(8,128)} fusion(f32[3,512,512]{2,1,0:T(8,128)S(1)} %fusion.6, f32[3,512,512]{2,1,0:T(8,128)S(1)} %fusion.53, f32[3]{0:T(128)S(1)} %get-tuple-element.5, f32[512,512]{1,0:T(8,128)S(1)} %fusion.20, pred[3]{0:T(512)(128)(4,1)S(1)} %fusion.32), kind=kOutput, calls=%fused_computation.3 | convolution fusion | flops 4834983936 | bytes 10485775 | tf_op jit(solution)/shard_map/bij,bjk->bik/dot_general | solution.py:125
  (11 shorter events, 0.1 us)
Async XLA Ops:
  36.3 30.5 %all-to-all-start = ((s32[16,2,5]{2,1,0:T(2,128)}), s32[16,2,5]{2,1,0:T(2,128)S(1)}, u32[]{:S(2)}, u32[]{:S(2)}) async-start(s32[16,2,5]{2,1,0:T(2,128)} %bitcast.12), calls=%async_computation | async-start | bytes 32768 | tf_op jit(solution)/shard_map/all_to_all | solution.py:94
  66.8 247.8 %all-to-all-start.2 = ((bf16[32,512,512]{2,1,0:T(8,128)(2,1)}), bf16[32,512,512]{2,1,0:T(8,128)(2,1)}, u32[]{:S(2)}, u32[]{:S(2)}) async-start(bf16[32,512,512]{2,1,0:T(8,128)(2,1)} %bitcast.60), calls=%async_computation.2 | async-start | bytes 33554432 | tf_op jit(solution)/shard_map/all_to_all | solution.py:93
  314.7 52.2 %all-to-all-start.1 = ((s32[8,3,5]{2,1,0:T(4,128)}), s32[8,3,5]{2,1,0:T(4,128)S(1)}, u32[]{:S(2)}, u32[]{:S(2)}) async-start(s32[8,3,5]{2,1,0:T(4,128)} %copy.32), calls=%async_computation.1 | async-start | bytes 32768 | tf_op jit(solution)/shard_map/all_to_all | solution.py:103
  366.9 5.4 copy-start
  366.9 166.2 %all-to-all-start.3 = ((bf16[24,512,512]{2,1,0:T(8,128)(2,1)}), bf16[24,512,512]{2,1,0:T(8,128)(2,1)}, u32[]{:S(2)}, u32[]{:S(2)}) async-start(bf16[24,512,512]{2,1,0:T(8,128)(2,1)} %bitcast.62), calls=%async_computation.3 | async-start | bytes 25165824 | tf_op jit(solution)/shard_map/all_to_all | solution.py:102
  550.3 5.7 copy-start.1
where the time goes:
time: 605 us; the launch traced here: 597 us
  waiting for transfers between devices  240 us (40%)
  blocking collectives  190 us (31%)
  matrix products  77.6 us (13%)
  local copies, waits for them, and re-layouts  52 us (9%)
  starting transfers between devices  22.8 us (4%)
  other arithmetic  13.9 us (2%)
    all_to_all x1, waiting for transfers between devices, shards(): lax.all_to_all(moved, COL, split_axis=0, concat_axis=0, tiled=True)  240 us
    psum x4, blocking collectives, over_axes(): return functools.reduce(lax.psum, axes, value)  158 us
    unnamed x9, local copies, waits for them, and re-layouts  51 us
    all_gather x4, blocking collectives, prefix_by_axis(): pieces = lax.all_gather(so_far, axis)  31.6 us
    dot_general x2, matrix products, bucket(): jnp.dot(chooser.astype(jnp.bfloat16), blocks.reshape(item_total, block_wi...  21.8 us
    dot_general x3, matrix products, shards(): root_iter = jnp.einsum('bij,bjk->bik', root_iter, step_mat, precision=HIGH)  18.3 us
    dot_general x2, matrix products, shards(): square_mat = jnp.einsum('bij,bjk->bik', step_mat, step_mat, precision=HIGH)  14.4 us
  transfers between devices with their start and end apart: 4, of which 1 were waited for; matrix products, arithmetic and copies ran while one was open for 13% of the time, Pallas kernels for 0%

commit v1 on v0

v1 whole, which is shorter than its diff:
```python
import functools

import jax
import jax.numpy as jnp
from jax import lax
from jax.experimental import pallas as pl
from jax.experimental.pallas import tpu as pltpu
from jax.sharding import Mesh
from jax.sharding import PartitionSpec as P

AXES = ("y", "c", "z", "x")
MESH = pl.DeviceIdType.MESH
DEVICES = 128
HALF = 256
CAP = 3
F32 = jnp.float32
BF16 = jnp.bfloat16


def iota(shape, dim):
    return lax.broadcasted_iota(jnp.int32, shape, dim)


def total(value):
    return jnp.sum(jnp.sum(value, axis=1, keepdims=True), axis=0, keepdims=True)


def peer(k, here):
    y, c, z, x = here
    k = (k * 37) & (DEVICES - 1)
    there = (
        (y + ((k >> 4) & 3)) & 3,
        (c + (k >> 6)) & 1,
        (z + ((k >> 2) & 3)) & 3,
        (x + (k & 3)) & 3,
    )
    return there, ((there[0] * 2 + there[1]) * 4 + there[2]) * 4 + there[3]


def pack(f_ref, t_ref, send1, meta):
    row, col = iota((HALF, HALF), 0), iota((HALF, HALF), 1)
    sq = jnp.zeros((1, 1), F32)
    diagonals = []
    for h in range(2):
        a = f_ref[h, 0:HALF, 0:HALF].astype(F32)
        b = f_ref[h, 0:HALF, HALF:]
        c = f_ref[h, HALF:, 0:HALF].astype(F32)
        d = f_ref[h, HALF:, HALF:].astype(F32)
        bf = b.astype(F32)
        sq = sq + total(a * a + bf * bf + c * c + d * d)
        v = jnp.where(row <= col, a, d).astype(BF16)
        diagonals.append(jnp.sum(jnp.where(row == col, d, 0.0), axis=0, keepdims=True))
        for part, w in enumerate((b, v)):
            for lanes in range(2):
                start = lanes * 64 + part * 32
                piece = w[:, lanes * 128 : lanes * 128 + 128]
                send1[h, start : start + 32] = piece.reshape(32, 8, 128)
    high = sq.astype(BF16).astype(F32)
    middle = (sq - high).astype(BF16).astype(F32)
    low = sq - high - middle
    line, lane = iota((8, 128), 0), iota((8, 128), 1)
    facts = jnp.zeros((8, 128), F32)
    words = (t_ref[0, 0].astype(F32), t_ref[1, 0].astype(F32), high, middle, low)
    for at, word in enumerate(words):
        facts = jnp.where(lane == at, word, facts)
    out = jnp.where(line == 4, facts, 0.0)
    for h in range(2):
        for lanes in range(2):
            piece = diagonals[h][:, lanes * 128 : lanes * 128 + 128]
            out = jnp.where(line == 2 * h + lanes, piece, out)
    meta[...] = out.astype(BF16)


def plan(me, all_meta, order, aux_ref):
    table = all_meta[...].reshape(DEVICES * 8, 128)
    pick = iota((DEVICES, DEVICES * 8), 1) == iota((DEVICES, DEVICES * 8), 0) * 8 + 4
    facts = jnp.dot(
        jnp.where(pick, 1.0, 0.0).astype(BF16), table, preferred_element_type=F32
    )
    across = facts.T
    t0, t1 = facts[:, 0:1], facts[:, 1:2]
    r0, r1 = across[0:1, :], across[1:2, :]
    sq = (across[2:3, :] + across[3:4, :]) + across[4:5, :]
    i, j = iota((DEVICES, DEVICES), 0), iota((DEVICES, DEVICES), 1)

    def same(a, b):
        return jnp.where(a == b, 1.0, 0.0)

    def along(value):
        return jnp.sum(value, axis=1, keepdims=True)

    before = j < i
    slot0 = along(jnp.where(before, same(r0, t0) + same(r1, t0), 0.0))
    slot1 = along(jnp.where(before, same(r0, t1) + same(r1, t1), 0.0)) + same(t0, t1)
    layer = along(jnp.where((i >> 4) == (j >> 4), sq, 0.0))
    fi, fj = i.astype(F32), j.astype(F32)
    line, lane = iota((8, 128), 0), iota((8, 128), 1)
    mine = iota((1, 128), 1) == me
    wanted = jnp.zeros((8, 128), F32)
    spots = jnp.full((8, 1), -1.0, F32)
    numbers = jnp.zeros((8, 128), F32)
    for s in range(CAP):
        first = jnp.where(t0 == fj, same(slot0, s), 0.0)
        second = jnp.where(t1 == fj, same(slot1, s), 0.0)
        both = first + second
        holds = jnp.sum(first * fi + second * (fi + DEVICES), axis=0, keepdims=True)
        filled = jnp.sum(both, axis=0, keepdims=True)
        layers = jnp.sum(both * layer, axis=0, keepdims=True)
        wanted = jnp.where(line == s, holds, wanted)
        my_block = along(jnp.where(mine, holds, 0.0))
        my_filled = along(jnp.where(mine, filled, 0.0))
        my_layer = along(jnp.where(mine, layers, 0.0))
        scale = 2.0 * jnp.sqrt(jnp.where(my_filled > 0, my_layer, 16384.0) / 16384.0)
        inverse = jnp.where(my_filled > 0, 1.0 / scale, 0.0)
        factor = jnp.where(my_filled > 0, lax.rsqrt(jnp.sqrt(scale)), 0.0)
        numbers = jnp.where((line == s) & (lane == 0), inverse, numbers)
        numbers = jnp.where((line == s) & (lane == 1), factor, numbers)
        late = jnp.where(my_block >= DEVICES, 1.0, 0.0)
        spot = (my_block - late * DEVICES) * 8.0 + late * 2.0
        for lanes in range(2):
            spots = jnp.where(iota((8, 1), 0) == 2 * s + lanes, spot + lanes, spots)
    order[...] = wanted.astype(jnp.int32)
    pick = iota((8, DEVICES * 8), 1).astype(F32) == spots
    aux_ref[0:8, :] = jnp.dot(
        jnp.where(pick, 1.0, 0.0).astype(BF16), table, preferred_element_type=F32
    )
    aux_ref[8:16, :] = numbers


def move_kernel(
    f_ref, t_ref, g_ref, aux_ref,
    send1, got1, meta, all_meta, send2, got2, order, order_s,
    meta_out, meta_in, out1, in1, out2, in2, local,
):
    here = tuple(lax.axis_index(a) for a in AXES)
    me = ((here[0] * 2 + here[1]) * 4 + here[2]) * 4 + here[3]
    barrier = pltpu.get_barrier_semaphore()

    @pl.loop(1, DEVICES)
    def _(k):
        there, _ = peer(k, here)
        pl.semaphore_signal(barrier, 1, device_id=there, device_id_type=MESH)

    pack(f_ref, t_ref, send1, meta)
    pl.semaphore_wait(barrier, DEVICES - 1)

    @pl.loop(1, DEVICES)
    def _(k):
        there, _ = peer(k, here)
        pltpu.make_async_remote_copy(
            src_ref=meta, dst_ref=all_meta.at[me], send_sem=meta_out, recv_sem=meta_in,
            device_id=there, device_id_type=MESH,
        ).start()

    @pl.loop(1, DEVICES)
    def _(k):
        there, index = peer(k, here)
        pltpu.make_async_remote_copy(
            src_ref=send1.at[:, index], dst_ref=got1.at[:, me], send_sem=out1, recv_sem=in1,
            device_id=there, device_id_type=MESH,
        ).start()

    all_meta[me] = meta[...]
    got1[:, me] = send1[:, me]

    def settle(buffer, *sems):
        for sem in sems:
            pltpu.make_async_copy(buffer, buffer, sem).wait()

    settle(all_meta.at[0 : DEVICES - 1], meta_in, meta_out)
    plan(me, all_meta, order, aux_ref)
    copy = pltpu.make_async_copy(order, order_s, local)
    copy.start()
    copy.wait()
    settle(got1.at[:, 0 : DEVICES - 1], in1, out1)
    for s in range(CAP):

        @pl.loop(0, DEVICES, unroll=8)
        def _(d, s=s):
            block = order_s[s, d]
            send2[s, d] = got1[(block >> 7) & 1, block & (DEVICES - 1)]

        @pl.loop(1, DEVICES)
        def _(k, s=s):
            there, index = peer(k, here)
            pltpu.make_async_remote_copy(
                src_ref=send2.at[s, index], dst_ref=got2.at[s, me], send_sem=out2.at[s], recv_sem=in2.at[s],
                device_id=there, device_id_type=MESH,
            ).start()

        got2[s, me] = send2[s, me]
    for s in range(CAP):
        settle(got2.at[s, 0 : DEVICES - 1], in2.at[s], out2.at[s])
        g_ref[s] = got2[s]


def move(factors, target):
    vmem, dma = pltpu.VMEM, pltpu.SemaphoreType.DMA
    return pl.pallas_call(
        move_kernel,
        out_shape=(
            jax.ShapeDtypeStruct((CAP, DEVICES, 8, 128), BF16),
            jax.ShapeDtypeStruct((16, 128), F32),
        ),
        in_specs=[pl.BlockSpec(memory_space=vmem), pl.BlockSpec(memory_space=pltpu.SMEM)],
        out_specs=[pl.BlockSpec(memory_space=vmem)] * 2,
        scratch_shapes=[
            vmem((2, DEVICES, 8, 128), BF16),
            vmem((2, DEVICES, 8, 128), BF16),
            vmem((8, 128), BF16),
            vmem((DEVICES, 8, 128), BF16),
            vmem((CAP, DEVICES, 8, 128), BF16),
            vmem((CAP, DEVICES, 8, 128), BF16),
            vmem((8, 128), jnp.int32),
            pltpu.SMEM((8, 128), jnp.int32),
            dma, dma, dma, dma, dma((CAP,)), dma((CAP,)), dma,
        ],
        compiler_params=pltpu.CompilerParams(collective_id=0, has_side_effects=True),
        name="move",
    )(factors, target)


def split(value):
    high = value.astype(BF16)
    return high, (value - high.astype(F32)).astype(BF16)


def dot(a, b):
    return jnp.dot(a, b, preferred_element_type=F32)


def product(left, right):
    return dot(left[0], right[0]) + (dot(left[0], right[1]) + dot(left[1], right[0]))


def root_kernel(g_ref, aux_ref, o_ref, block):
    s = pl.program_id(0)
    row, col = iota((HALF, HALF), 0), iota((HALF, HALF), 1)

    def whole(part):
        return jnp.concatenate(
            [
                g_ref[0, lanes * 64 + part * 32 : lanes * 64 + part * 32 + 32].reshape(HALF, 128)
                for lanes in range(2)
            ],
            axis=1,
        )

    u = whole(0)
    v = whole(1).astype(F32)
    flipped = v.T
    diagonal = jnp.concatenate(
        [aux_ref[pl.ds(2 * s, 1), :], aux_ref[pl.ds(2 * s + 1, 1), :]], axis=1
    )
    block[0:HALF, 0:HALF] = jnp.where(row <= col, v, flipped).astype(BF16)
    block[0:HALF, HALF:] = u
    block[HALF:, 0:HALF] = u.astype(F32).T.astype(BF16)
    corner = jnp.where(row > col, v, jnp.where(row == col, diagonal, flipped))
    block[HALF:, HALF:] = corner.astype(BF16)
    inverse = aux_ref[pl.ds(8 + s, 1), 0:1]
    factor = aux_ref[pl.ds(8 + s, 1), 1:2]
    eye = jnp.where(iota((512, 512), 0) == iota((512, 512), 1), 1.25, 0.0)

    a = block[...]
    q = inverse * 0.25
    af = a.astype(F32)
    square = (1.25 * eye - (2.5 * q) * af) + (dot(a, a) * q) * q
    square = split(square)
    fifth = split((dot(square[0], a) + dot(square[1], a)) * q)
    step = eye - product(square, fifth)
    parts = split(step)
    square = product(parts, parts)
    rest = split(1.25 * step - square)
    square = split(square)
    rest = split(product(square, rest))
    both = 1.25 * step - product(square, rest)
    parts = split(both)
    out = 1.25 * both - (dot(parts[0], a) + dot(parts[1], a)) * q
    o_ref[0] = out * factor


def roots(moved, aux):
    return pl.pallas_call(
        root_kernel,
        grid=(CAP,),
        out_shape=jax.ShapeDtypeStruct((CAP, 512, 512), F32),
        in_specs=[
            pl.BlockSpec((1, DEVICES, 8, 128), lambda s: (s, 0, 0, 0)),
            pl.BlockSpec((16, 128), lambda s: (0, 0)),
        ],
        out_specs=pl.BlockSpec((1, 512, 512), lambda s: (s, 0, 0)),
        scratch_shapes=[pltpu.VMEM((512, 512), BF16)],
        name="roots",
    )(moved, aux)


def shards(factors, target):
    moved, aux = move(factors[0], target)
    return roots(moved, aux)[None]


def solution(mesh):
    finer = Mesh(mesh.devices.reshape(4, 2, 4, 4), AXES)
    placed = (P(AXES, None, None, None), P(AXES, None))
    return jax.shard_map(
        shards, mesh=finer, in_specs=placed, out_specs=P(AXES, None, None, None), check_vma=False
    )
```

time: 605 us -> 60.2 us (0.10); the launches traced: 597 us -> 60 us
  waiting for transfers between devices: 240 us -> 0 us
  blocking collectives: 190 us -> 0 us
  matrix products: 77.6 us -> 0 us
  Pallas kernels: 0 us -> 58.7 us
  local copies, waits for them, and re-layouts: 52 us -> 1.3 us
  starting transfers between devices: 22.8 us -> 0 us
  other arithmetic: 13.9 us -> 0 us
    all_to_all x4 -> x0, waiting for transfers between devices: 240 us -> none  [the longest x1 240 us: shards(): lax.all_to_all(moved, COL, split_axis=0, concat_axis=0, tiled=True)]
    psum x4 -> x0, blocking collectives: 158 us -> none  [over_axes(): return functools.reduce(lax.psum, axes, value)]
    dot_general x13 -> x0, matrix products: 77.6 us -> none  [the longest x2 21.8 us: bucket(): jnp.dot(chooser.astype(jnp.bfloat16), blocks.reshape(item_total, block_wi...]
    pallas_call x0 -> x2, Pallas kernels: none -> 58.7 us  [the longest x1 41.2 us: move(): pl.pallas_call(move_kernel, out_shape=(jax.ShapeDtypeStruct((CAP, DEVICES...]
    unnamed x9 -> x1, local copies, waits for them, and re-layouts: 51 us -> 1.3 us
    all_gather x4 -> x0, blocking collectives: 31.6 us -> none  [prefix_by_axis(): pieces = lax.all_gather(so_far, axis)]
    all_to_all x4 -> x0, starting transfers between devices: 22.8 us -> none  [the longest x1 7.21 us: shards(): lax.all_to_all(as_sent(moved_labels), ROW, split_axis=0, concat_axis=0, t...]
    reduce_sum x6 -> x0, other arithmetic: 11.3 us -> none  [the longest x1 8.36 us: shards(): jnp.sum(moved.reshape(row_count, CAP, block_width, block_width).astype(jn...]
  transfers between devices with their start and end apart: 4 -> 0, of which waited for: 1 -> 0; matrix products, arithmetic and copies ran while one was open for 13% -> 0% of each run, Pallas kernels for 0% -> 0%
where the time goes in v1:
time: 60.2 us; the launch traced here: 60 us
  Pallas kernels  58.7 us (98%)
  local copies, waits for them, and re-layouts  1.3 us (2%)
    pallas_call x1, Pallas kernels, move(): pl.pallas_call(move_kernel, out_shape=(jax.ShapeDtypeStruct((CAP, DEVICES...  41.2 us
    pallas_call x1, Pallas kernels, roots(): pl.pallas_call(root_kernel, grid=(CAP,), out_shape=jax.ShapeDtypeStruct((...  17.6 us
    unnamed x1, local copies, waits for them, and re-layouts  1.3 us

profile of v1, /device:TPU:1, one launch (start us, length us, event | category | flops | bytes accessed | tf_op | source)
XLA Modules:
  0.0 60.0 jit_solution(3721073841986434460)
XLA Ops:
  0.0 1.3 %copy.3.t_ref = s32[2,1]{1,0:T(2,128)} copy(s32[2,1]{0,1:T(1,128)} %param.3) | data formatting | bytes 16 | tf_op args[1]
  1.3 41.2 %move.1 = (bf16[3,128,8,128]{3,2,1,0:T(8,128)(2,1)}, f32[16,128]{1,0:T(8,128)}) custom-call(bf16[2,512,512]{2,1,0:T(8,128)(2,1)} %bitcast.2, s32[2,1]{1,0:T(2,128)} %copy.3.t_ref), custom_call_target="tpu_custom_call" | custom-call | tf_op jit(solution)/shard_map/move/pallas_call | solution.py:199
  42.5 17.6 %roots.1 = f32[3,512,512]{2,1,0:T(8,128)} custom-call(bf16[3,128,8,128]{3,2,1,0:T(8,128)(2,1)} %get-tuple-element.7.g_ref, f32[16,128]{1,0:T(8,128)} %get-tuple-element.8.aux_ref), custom_call_target="tpu_custom_call" | custom-call | tf_op jit(solution)/shard_map/roots/pallas_call | solution.py:283

commit v2 on v1

v2 whole, which is shorter than its diff:
```python
import functools

import jax
import jax.numpy as jnp
from jax import lax
from jax.experimental import pallas as pl
from jax.experimental.pallas import tpu as pltpu
from jax.sharding import Mesh
from jax.sharding import PartitionSpec as P

AXES = ("y", "c", "z", "x")
MESH = pl.DeviceIdType.MESH
DEVICES = 128
HALF = 256
CAP = 3
F32 = jnp.float32
BF16 = jnp.bfloat16


def iota(shape, dim):
    return lax.broadcasted_iota(jnp.int32, shape, dim)


def total(value):
    return jnp.sum(jnp.sum(value, axis=1, keepdims=True), axis=0, keepdims=True)


def peer(k, here):
    y, c, z, x = here
    k = (k * 37) & (DEVICES - 1)
    there = (
        (y + ((k >> 4) & 3)) & 3,
        (c + (k >> 6)) & 1,
        (z + ((k >> 2) & 3)) & 3,
        (x + (k & 3)) & 3,
    )
    return there, ((there[0] * 2 + there[1]) * 4 + there[2]) * 4 + there[3]


def each_peer(here, do):
    for start, stop, unroll in ((1, 8, 7), (8, DEVICES, 8)):

        @pl.loop(start, stop, unroll=unroll)
        def _(k):
            do(*peer(k, here))


def pack(f_ref, t_ref, send1, facts_ref, diagonal_ref):
    row, col = iota((HALF, HALF), 0), iota((HALF, HALF), 1)
    sq = jnp.zeros((1, 1), F32)
    line = iota((2, 128), 0)
    for h in range(2):
        a = f_ref[h, 0:HALF, 0:HALF].astype(F32)
        b = f_ref[h, 0:HALF, HALF:]
        c = f_ref[h, HALF:, 0:HALF].astype(F32)
        d = f_ref[h, HALF:, HALF:].astype(F32)
        bf = b.astype(F32)
        sq = sq + total(a * a + bf * bf + c * c + d * d)
        v = jnp.where(row <= col, a, d).astype(BF16)
        diagonal = jnp.sum(jnp.where(row == col, d, 0.0), axis=0, keepdims=True)
        diagonal = jnp.where(line == 0, diagonal[:, 0:128], diagonal[:, 128:])
        diagonal_ref[h] = diagonal.astype(BF16)
        for part, w in enumerate((b, v)):
            for lanes in range(2):
                start = lanes * 64 + part * 32
                piece = w[:, lanes * 128 : lanes * 128 + 128]
                send1[h, start : start + 32] = piece.reshape(32, 8, 128)
    lane = iota((1, 128), 1)
    facts = jnp.where(lane == 0, t_ref[0:1, 0:1].astype(F32), 0.0)
    facts = jnp.where(lane == 1, t_ref[1:2, 0:1].astype(F32), facts)
    facts_ref[...] = jnp.where(lane == 2, sq, facts)


def plan(me, all_facts, order, aux_ref):
    facts = all_facts[:, 0, :]
    across = facts.T
    t0, t1 = facts[:, 0:1], facts[:, 1:2]
    r0, r1, sq = across[0:1, :], across[1:2, :], across[2:3, :]
    i, j = iota((DEVICES, DEVICES), 0), iota((DEVICES, DEVICES), 1)

    def same(a, b):
        return jnp.where(a == b, 1.0, 0.0)

    def along(value):
        return jnp.sum(value, axis=1, keepdims=True)

    before = j < i
    slot0 = along(jnp.where(before, same(r0, t0) + same(r1, t0), 0.0))
    slot1 = along(jnp.where(before, same(r0, t1) + same(r1, t1), 0.0)) + same(t0, t1)
    layer = along(jnp.where((i >> 4) == (j >> 4), sq, 0.0))
    fi, fj = i.astype(F32), j.astype(F32)
    line, lane = iota((8, 128), 0), iota((8, 128), 1)
    mine = iota((1, 128), 1) == me
    wanted = jnp.zeros((8, 128), F32)
    numbers = jnp.zeros((8, 128), F32)
    for s in range(CAP):
        first = jnp.where(t0 == fj, same(slot0, s), 0.0)
        second = jnp.where(t1 == fj, same(slot1, s), 0.0)
        both = first + second
        holds = jnp.sum(first * fi + second * (fi + DEVICES), axis=0, keepdims=True)
        filled = jnp.sum(both, axis=0, keepdims=True)
        layers = jnp.sum(both * layer, axis=0, keepdims=True)
        wanted = jnp.where(line == s, holds, wanted)
        my_filled = along(jnp.where(mine, filled, 0.0))
        my_layer = along(jnp.where(mine, layers, 0.0))
        scale = 2.0 * jnp.sqrt(jnp.where(my_filled > 0, my_layer, 16384.0) / 16384.0)
        inverse = jnp.where(my_filled > 0, 1.0 / scale, 0.0)
        factor = jnp.where(my_filled > 0, lax.rsqrt(jnp.sqrt(scale)), 0.0)
        numbers = jnp.where((line == s) & (lane == 0), inverse, numbers)
        numbers = jnp.where((line == s) & (lane == 1), factor, numbers)
    order[...] = wanted.astype(jnp.int32)
    aux_ref[8:16, :] = numbers


def move_kernel(
    f_any, t_ref, g_ref, aux_ref,
    f_ref, send1, got1, facts, all_facts, diagonal, all_diagonal, send2, got2, order, order_s,
    facts_out, facts_in, diagonal_out, diagonal_in, out1, in1, out2, in2, local,
):
    here = tuple(lax.axis_index(a) for a in AXES)
    me = ((here[0] * 2 + here[1]) * 4 + here[2]) * 4 + here[3]
    load = pltpu.make_async_copy(f_any, f_ref, local)
    load.start()
    barrier = pltpu.get_barrier_semaphore()
    each_peer(
        here,
        lambda there, _: pl.semaphore_signal(barrier, 1, device_id=there, device_id_type=MESH),
    )
    load.wait()
    pack(f_ref, t_ref, send1, facts, diagonal)
    pl.semaphore_wait(barrier, DEVICES - 1)

    def send(source, target, gone, came):
        def start(there, index):
            pltpu.make_async_remote_copy(
                src_ref=source(index), dst_ref=target, send_sem=gone, recv_sem=came,
                device_id=there, device_id_type=MESH,
            ).start()

        each_peer(here, start)

    def settle(buffer, *sems):
        for sem in sems:
            pltpu.make_async_copy(buffer, buffer, sem).wait()

    send(lambda index: facts, all_facts.at[me], facts_out, facts_in)
    send(lambda index: send1.at[:, index], got1.at[:, me], out1, in1)
    send(lambda index: diagonal, all_diagonal.at[:, me], diagonal_out, diagonal_in)
    all_facts[me] = facts[...]
    got1[:, me] = send1[:, me]
    all_diagonal[:, me] = diagonal[...]
    settle(all_facts.at[0 : DEVICES - 1], facts_in, facts_out)
    plan(me, all_facts, order, aux_ref)
    copy = pltpu.make_async_copy(order, order_s, local)
    copy.start()
    copy.wait()
    settle(got1.at[:, 0 : DEVICES - 1], in1, out1)

    def place(block):
        return (block >> 7) & 1, block & (DEVICES - 1)

    for s in range(CAP):

        @pl.loop(0, DEVICES, unroll=8)
        def _(d, s=s):
            send2[s, d] = got1[place(order_s[s, d])]

        send(lambda index, s=s: send2.at[s, index], got2.at[s, me], out2.at[s], in2.at[s])
        got2[s, me] = send2[s, me]
    settle(all_diagonal.at[:, 0 : DEVICES - 1], diagonal_in, diagonal_out)
    for s in range(CAP):
        aux_ref[2 * s : 2 * s + 2, :] = all_diagonal[place(order_s[s, me])].astype(F32)
        settle(got2.at[s, 0 : DEVICES - 1], in2.at[s], out2.at[s])
        g_ref[s] = got2[s]


def move(factors, target):
    vmem, dma = pltpu.VMEM, pltpu.SemaphoreType.DMA
    return pl.pallas_call(
        move_kernel,
        out_shape=(
            jax.ShapeDtypeStruct((CAP, DEVICES, 8, 128), BF16),
            jax.ShapeDtypeStruct((16, 128), F32),
        ),
        in_specs=[pl.BlockSpec(memory_space=pl.ANY), pl.BlockSpec(memory_space=vmem)],
        out_specs=[pl.BlockSpec(memory_space=vmem)] * 2,
        scratch_shapes=[
            vmem((2, 512, 512), BF16),
            vmem((2, DEVICES, 8, 128), BF16),
            vmem((2, DEVICES, 8, 128), BF16),
            vmem((1, 128), F32),
            vmem((DEVICES, 1, 128), F32),
            vmem((2, 2, 128), BF16),
            vmem((2, DEVICES, 2, 128), BF16),
            vmem((CAP, DEVICES, 8, 128), BF16),
            vmem((CAP, DEVICES, 8, 128), BF16),
            vmem((8, 128), jnp.int32),
            pltpu.SMEM((8, 128), jnp.int32),
            dma, dma, dma, dma, dma, dma, dma((CAP,)), dma((CAP,)), dma,
        ],
        compiler_params=pltpu.CompilerParams(collective_id=0, has_side_effects=True),
        name="move",
    )(factors, target)


def dot(a, b):
    return jnp.dot(a, b, preferred_element_type=F32)


LEFT, RIGHT = slice(0, HALF), slice(HALF, 2 * HALF)


def tiles(ref):
    return [ref[r, c].astype(F32) for r, c in ((LEFT, LEFT), (LEFT, RIGHT), (RIGHT, RIGHT))]


def product(*pairs):
    right = sum(dot(a[...], b[:, RIGHT]) for a, b in pairs)
    corner = sum(dot(a[LEFT, :], b[:, LEFT]) for a, b in pairs)
    return [corner, right[LEFT], right[RIGHT]]


def times(a, b):
    return product((a[0], b[0]), (a[0], b[1]), (a[1], b[0]))


def keep(ref, value):
    places = (LEFT, LEFT), (LEFT, RIGHT), (RIGHT, RIGHT), (RIGHT, LEFT)
    for (r, c), tile in zip(places, (*value, value[1].T)):
        high = tile.astype(BF16)
        ref[0, r, c] = high
        ref[1, r, c] = (tile - high.astype(F32)).astype(BF16)


def unfold(g, diagonal, block):
    row, col = iota((HALF, HALF), 0), iota((HALF, HALF), 1)

    def whole(part):
        return jnp.concatenate(
            [
                g[lanes * 64 + part * 32 : lanes * 64 + part * 32 + 32].reshape(HALF, 128)
                for lanes in range(2)
            ],
            axis=1,
        )

    u = whole(0)
    v = whole(1).astype(F32)
    flipped = v.T
    block[LEFT, LEFT] = jnp.where(row <= col, v, flipped).astype(BF16)
    block[LEFT, RIGHT] = u
    block[RIGHT, LEFT] = u.astype(F32).T.astype(BF16)
    corner = jnp.where(row > col, v, jnp.where(row == col, diagonal, flipped))
    block[RIGHT, RIGHT] = corner.astype(BF16)


def newton(block, inverse, factor, out, x, y, z):
    eye = jnp.where(iota((HALF, HALF), 0) == iota((HALF, HALF), 1), 1.25, 0.0)
    eyes = (eye, 0.0, eye)
    q = inverse * 0.25
    square = product((block, block))
    keep(x, [1.25 * e - (2.5 * q) * a + (s * q) * q for e, a, s in zip(eyes, tiles(block), square)])
    keep(y, [t * q for t in product((x.at[0], block), (x.at[1], block))])
    step = [e - t for e, t in zip(eyes, times(x, y))]
    keep(z, step)
    square = times(z, z)
    keep(x, square)
    keep(y, [1.25 * t - s for t, s in zip(step, square)])
    keep(z, times(x, y))
    both = [1.25 * t - f for t, f in zip(step, times(x, z))]
    keep(y, both)
    rest = product((y.at[0], block), (y.at[1], block))
    root = [(1.25 * t - r * q) * factor for t, r in zip(both, rest)]
    out[LEFT, LEFT] = root[0]
    out[LEFT, RIGHT] = root[1]
    out[RIGHT, RIGHT] = root[2]
    out[RIGHT, LEFT] = root[1].T


def root_kernel(g_ref, aux_ref, o_ref, block, x, y, z):
    s = pl.program_id(0)
    diagonal = jnp.concatenate(
        [aux_ref[pl.ds(2 * s, 1), :], aux_ref[pl.ds(2 * s + 1, 1), :]], axis=1
    )
    unfold(g_ref.at[0], diagonal, block)
    inverse = aux_ref[pl.ds(8 + s, 1), 0:1]
    factor = aux_ref[pl.ds(8 + s, 1), 1:2]
    newton(block, inverse, factor, o_ref.at[0], x, y, z)


def roots(moved, aux):
    return pl.pallas_call(
        root_kernel,
        grid=(CAP,),
        out_shape=jax.ShapeDtypeStruct((CAP, 512, 512), F32),
        in_specs=[
            pl.BlockSpec((1, DEVICES, 8, 128), lambda s: (s, 0, 0, 0)),
            pl.BlockSpec((16, 128), lambda s: (0, 0)),
        ],
        out_specs=pl.BlockSpec((1, 512, 512), lambda s: (s, 0, 0)),
        scratch_shapes=[pltpu.VMEM((512, 512), BF16)] + [pltpu.VMEM((2, 512, 512), BF16)] * 3,
        name="roots",
    )(moved, aux)


def shards(factors, target):
    moved, aux = move(factors[0], target)
    return roots(moved, aux)[None]


def solution(mesh):
    finer = Mesh(mesh.devices.reshape(4, 2, 4, 4), AXES)
    placed = (P(AXES, None, None, None), P(AXES, None))
    return jax.shard_map(
        shards, mesh=finer, in_specs=placed, out_specs=P(AXES, None, None, None), check_vma=False
    )
```

time: 60.2 us -> 57.1 us (0.949)
  Pallas kernels: 58.7 us -> 55.6 us
    pallas_call x1, Pallas kernels: 41.2 us -> 38.1 us  [move(): pl.pallas_call(move_kernel, out_shape=(jax.ShapeDtypeStruct((CAP, DEVICES...]
where the time goes in v2:
time: 57.1 us; the launch traced here: 56.9 us
  Pallas kernels  55.6 us (97%)
  local copies, waits for them, and re-layouts  1.3 us (2%)
    pallas_call x1, Pallas kernels, move(): pl.pallas_call(move_kernel, out_shape=(jax.ShapeDtypeStruct((CAP, DEVICES...  38.1 us
    pallas_call x1, Pallas kernels, roots(): pl.pallas_call(root_kernel, grid=(CAP,), out_shape=jax.ShapeDtypeStruct((...  17.5 us
    unnamed x1, local copies, waits for them, and re-layouts  1.3 us

profile of v2, /device:TPU:1, one launch (start us, length us, event | category | flops | bytes accessed | tf_op | source)
XLA Modules:
  0.0 56.9 jit_solution(3550052792186315703)
XLA Ops:
  0.0 1.3 %copy.3.t_ref = s32[2,1]{1,0:T(2,128)} copy(s32[2,1]{0,1:T(1,128)} %param.3) | data formatting | bytes 16 | tf_op args[1]
  1.3 38.1 %move.1 = (bf16[3,128,8,128]{3,2,1,0:T(8,128)(2,1)}, f32[16,128]{1,0:T(8,128)}) custom-call(bf16[2,512,512]{2,1,0:T(8,128)(2,1)} %bitcast.2, s32[2,1]{1,0:T(2,128)} %copy.3.t_ref), custom_call_target="tpu_custom_call" | custom-call | tf_op jit(solution)/shard_map/move/pallas_call | solution.py:179
  39.4 17.5 %roots.1 = f32[3,512,512]{2,1,0:T(8,128)} custom-call(bf16[3,128,8,128]{3,2,1,0:T(8,128)(2,1)} %get-tuple-element.7.g_ref, f32[16,128]{1,0:T(8,128)} %get-tuple-element.8.aux_ref), custom_call_target="tpu_custom_call" | custom-call | tf_op jit(solution)/shard_map/roots/pallas_call | solution.py:292

commit v3 on v2

--- a/solution.py
+++ b/solution.py
@@ -1,4 +1,4 @@
-import functools
+import itertools
 
 import jax
 import jax.numpy as jnp
@@ -112,9 +112,95 @@
     aux_ref[8:16, :] = numbers
 
 
+def dot(a, b):
+    return jnp.dot(a, b, preferred_element_type=F32)
+
+
+LEFT, RIGHT = slice(0, HALF), slice(HALF, 2 * HALF)
+
+
+def tiles(ref):
+    return [ref[r, c].astype(F32) for r, c in ((LEFT, LEFT), (LEFT, RIGHT), (RIGHT, RIGHT))]
+
+
+def product(*pairs):
+    right = sum(dot(a[...], b[:, RIGHT]) for a, b in pairs)
+    corner = sum(dot(a[LEFT, :], b[:, LEFT]) for a, b in pairs)
+    return [corner, right[LEFT], right[RIGHT]]
+
+
+def times(a, b):
+    return product((a[0], b[0]), (a[0], b[1]), (a[1], b[0]))
+
+
+def keep(ref, value):
+    places = (LEFT, LEFT), (LEFT, RIGHT), (RIGHT, RIGHT), (RIGHT, LEFT)
+    for (r, c), tile in zip(places, (*value, value[1].T)):
+        high = tile.astype(BF16)
+        ref[0, r, c] = high
+        ref[1, r, c] = (tile - high.astype(F32)).astype(BF16)
+
+
+def unfold(g, diagonal, block):
+    row, col = iota((HALF, HALF), 0), iota((HALF, HALF), 1)
+
+    def whole(part):
+        return jnp.concatenate(
+            [
+                g[lanes * 64 + part * 32 : lanes * 64 + part * 32 + 32].reshape(HALF, 128)
+                for lanes in range(2)
+            ],
+            axis=1,
+        )
+
+    u = whole(0)
+    v = whole(1).astype(F32)
+    flipped = v.T
+    block[LEFT, LEFT] = jnp.where(row <= col, v, flipped).astype(BF16)
+    block[LEFT, RIGHT] = u
+    block[RIGHT, LEFT] = u.astype(F32).T.astype(BF16)
+    corner = jnp.where(row > col, v, jnp.where(row == col, diagonal, flipped))
+    block[RIGHT, RIGHT] = corner.astype(BF16)
+
+
+def newton(block, inverse, factor, out, x, y, z):
+    eye = jnp.where(iota((HALF, HALF), 0) == iota((HALF, HALF), 1), 1.25, 0.0)
+    eyes = (eye, 0.0, eye)
+    q = inverse * 0.25
+    square = product((block, block))
+    keep(x, [1.25 * e - (2.5 * q) * a + (s * q) * q for e, a, s in zip(eyes, tiles(block), square)])
+    yield
+    keep(y, [t * q for t in product((x.at[0], block), (x.at[1], block))])
+    yield
+    step = [e - t for e, t in zip(eyes, times(x, y))]
+    keep(z, step)
+    yield
+    square = times(z, z)
+    keep(x, square)
+    keep(y, [1.25 * t - s for t, s in zip(step, square)])
+    yield
+    keep(z, times(x, y))
+    yield
+    both = [1.25 * t - f for t, f in zip(step, times(x, z))]
+    keep(y, both)
+    yield
+    rest = product((y.at[0], block), (y.at[1], block))
+    root = [(1.25 * t - r * q) * factor for t, r in zip(both, rest)]
+    out[LEFT, LEFT] = root[0]
+    out[LEFT, RIGHT] = root[1]
+    out[RIGHT, RIGHT] = root[2]
+    out[RIGHT, LEFT] = root[1].T
+
+
+def begin(s, g, aux_ref, out, block, x, y, z):
+    unfold(g, jnp.concatenate([aux_ref[2 * s : 2 * s + 1], aux_ref[2 * s + 1 : 2 * s + 2]], axis=1), block)
+    return newton(block, aux_ref[8 + s : 9 + s, 0:1], aux_ref[8 + s : 9 + s, 1:2], out, x, y, z)
+
+
 def move_kernel(
-    f_any, t_ref, g_ref, aux_ref,
+    f_any, t_ref, g_ref, aux_ref, out_any,
     f_ref, send1, got1, facts, all_facts, diagonal, all_diagonal, send2, got2, order, order_s,
+    root, block, x, y, z,
     facts_out, facts_in, diagonal_out, diagonal_in, out1, in1, out2, in2, local,
 ):
     here = tuple(lax.axis_index(a) for a in AXES)
@@ -170,8 +256,15 @@
     settle(all_diagonal.at[:, 0 : DEVICES - 1], diagonal_in, diagonal_out)
     for s in range(CAP):
         aux_ref[2 * s : 2 * s + 2, :] = all_diagonal[place(order_s[s, me])].astype(F32)
+    settle(got2.at[0, 0 : DEVICES - 1], in2.at[0], out2.at[0])
+    for _ in begin(0, got2.at[0], aux_ref, root, block, x, y, z):
+        pass
+    done = pltpu.make_async_copy(root, out_any, local)
+    done.start()
+    for s in range(1, CAP):
         settle(got2.at[s, 0 : DEVICES - 1], in2.at[s], out2.at[s])
-        g_ref[s] = got2[s]
+        g_ref[s - 1] = got2[s]
+    done.wait()
 
 
 def move(factors, target):
@@ -179,11 +272,12 @@
     return pl.pallas_call(
         move_kernel,
         out_shape=(
-            jax.ShapeDtypeStruct((CAP, DEVICES, 8, 128), BF16),
+            jax.ShapeDtypeStruct((CAP - 1, DEVICES, 8, 128), BF16),
             jax.ShapeDtypeStruct((16, 128), F32),
+            jax.ShapeDtypeStruct((512, 512), F32),
         ),
         in_specs=[pl.BlockSpec(memory_space=pl.ANY), pl.BlockSpec(memory_space=vmem)],
-        out_specs=[pl.BlockSpec(memory_space=vmem)] * 2,
+        out_specs=[pl.BlockSpec(memory_space=vmem)] * 2 + [pl.BlockSpec(memory_space=pl.ANY)],
         scratch_shapes=[
             vmem((2, 512, 512), BF16),
             vmem((2, DEVICES, 8, 128), BF16),
@@ -196,6 +290,11 @@
             vmem((CAP, DEVICES, 8, 128), BF16),
             vmem((8, 128), jnp.int32),
             pltpu.SMEM((8, 128), jnp.int32),
+            vmem((512, 512), F32),
+            vmem((512, 512), BF16),
+            vmem((2, 512, 512), BF16),
+            vmem((2, 512, 512), BF16),
+            vmem((2, 512, 512), BF16),
             dma, dma, dma, dma, dma, dma, dma((CAP,)), dma((CAP,)), dma,
         ],
         compiler_params=pltpu.CompilerParams(collective_id=0, has_side_effects=True),
@@ -203,109 +302,49 @@
     )(factors, target)
 
 
-def dot(a, b):
-    return jnp.dot(a, b, preferred_element_type=F32)
-
-
-LEFT, RIGHT = slice(0, HALF), slice(HALF, 2 * HALF)
-
-
-def tiles(ref):
-    return [ref[r, c].astype(F32) for r, c in ((LEFT, LEFT), (LEFT, RIGHT), (RIGHT, RIGHT))]
-
-
-def product(*pairs):
-    right = sum(dot(a[...], b[:, RIGHT]) for a, b in pairs)
-    corner = sum(dot(a[LEFT, :], b[:, LEFT]) for a, b in pairs)
-    return [corner, right[LEFT], right[RIGHT]]
-
-
-def times(a, b):
-    return product((a[0], b[0]), (a[0], b[1]), (a[1], b[0]))
-
-
-def keep(ref, value):
-    places = (LEFT, LEFT), (LEFT, RIGHT), (RIGHT, RIGHT), (RIGHT, LEFT)
-    for (r, c), tile in zip(places, (*value, value[1].T)):
-        high = tile.astype(BF16)
-        ref[0, r, c] = high
-        ref[1, r, c] = (tile - high.astype(F32)).astype(BF16)
-
-
-def unfold(g, diagonal, block):
-    row, col = iota((HALF, HALF), 0), iota((HALF, HALF), 1)
-
-    def whole(part):
-        return jnp.concatenate(
-            [
-                g[lanes * 64 + part * 32 : lanes * 64 + part * 32 + 32].reshape(HALF, 128)
-                for lanes in range(2)
-            ],
-            axis=1,
-        )
-
-    u = whole(0)
-    v = whole(1).astype(F32)
-    flipped = v.T
-    block[LEFT, LEFT] = jnp.where(row <= col, v, flipped).astype(BF16)
-    block[LEFT, RIGHT] = u
-    block[RIGHT, LEFT] = u.astype(F32).T.astype(BF16)
-    corner = jnp.where(row > col, v, jnp.where(row == col, diagonal, flipped))
-    block[RIGHT, RIGHT] = corner.astype(BF16)
-
-
-def newton(block, inverse, factor, out, x, y, z):
-    eye = jnp.where(iota((HALF, HALF), 0) == iota((HALF, HALF), 1), 1.25, 0.0)
-    eyes = (eye, 0.0, eye)
-    q = inverse * 0.25
-    square = product((block, block))
-    keep(x, [1.25 * e - (2.5 * q) * a + (s * q) * q for e, a, s in zip(eyes, tiles(block), square)])
-    keep(y, [t * q for t in product((x.at[0], block), (x.at[1], block))])
-    step = [e - t for e, t in zip(eyes, times(x, y))]
-    keep(z, step)
-    square = times(z, z)
-    keep(x, square)
-    keep(y, [1.25 * t - s for t, s in zip(step, square)])
-    keep(z, times(x, y))
-    both = [1.25 * t - f for t, f in zip(step, times(x, z))]
-    keep(y, both)
-    rest = product((y.at[0], block), (y.at[1], block))
-    root = [(1.25 * t - r * q) * factor for t, r in zip(both, rest)]
-    out[LEFT, LEFT] = root[0]
-    out[LEFT, RIGHT] = root[1]
-    out[RIGHT, RIGHT] = root[2]
-    out[RIGHT, LEFT] = root[1].T
-
-
-def root_kernel(g_ref, aux_ref, o_ref, block, x, y, z):
-    s = pl.program_id(0)
-    diagonal = jnp.concatenate(
-        [aux_ref[pl.ds(2 * s, 1), :], aux_ref[pl.ds(2 * s + 1, 1), :]], axis=1
-    )
-    unfold(g_ref.at[0], diagonal, block)
-    inverse = aux_ref[pl.ds(8 + s, 1), 0:1]
-    factor = aux_ref[pl.ds(8 + s, 1), 1:2]
-    newton(block, inverse, factor, o_ref.at[0], x, y, z)
-
-
-def roots(moved, aux):
+def root_kernel(g_ref, aux_ref, first_any, out_any, root, block, x, y, z, sems):
+    load = pltpu.make_async_copy(first_any, root.at[0], sems.at[0])
+    load.start()
+    works = [
+        begin(s, g_ref.at[s - 1], aux_ref, root.at[s], *(r.at[s - 1] for r in (block, x, y, z)))
+        for s in range(1, CAP)
+    ]
+    copies = [pltpu.make_async_copy(root.at[s], out_any.at[s], sems.at[s]) for s in range(CAP)]
+    for step, _ in enumerate(itertools.zip_longest(*works)):
+        if step == 3:
+            load.wait()
+            copies[0].start()
+    for copy in copies[1:]:
+        copy.start()
+    for copy in copies:
+        copy.wait()
+
+
+def roots(moved, aux, first):
+    vmem = pltpu.VMEM
     return pl.pallas_call(
         root_kernel,
-        grid=(CAP,),
         out_shape=jax.ShapeDtypeStruct((CAP, 512, 512), F32),
         in_specs=[
-            pl.BlockSpec((1, DEVICES, 8, 128), lambda s: (s, 0, 0, 0)),
-            pl.BlockSpec((16, 128), lambda s: (0, 0)),
+            pl.BlockSpec(memory_space=vmem),
+            pl.BlockSpec(memory_space=vmem),
+            pl.BlockSpec(memory_space=pl.ANY),
         ],
-        out_specs=pl.BlockSpec((1, 512, 512), lambda s: (s, 0, 0)),
-        scratch_shapes=[pltpu.VMEM((512, 512), BF16)] + [pltpu.VMEM((2, 512, 512), BF16)] * 3,
+        out_specs=pl.BlockSpec(memory_space=pl.ANY),
+        scratch_shapes=[
+            vmem((CAP, 512, 512), F32),
+            vmem((CAP - 1, 512, 512), BF16),
+            vmem((CAP - 1, 2, 512, 512), BF16),
+            vmem((CAP - 1, 2, 512, 512), BF16),
+            vmem((CAP - 1, 2, 512, 512), BF16),
+            pltpu.SemaphoreType.DMA((CAP,)),
+        ],
         name="roots",
-    )(moved, aux)
+    )(moved, aux, first)
 
 
 def shards(factors, target):
-    moved, aux = move(factors[0], target)
-    return roots(moved, aux)[None]
+    return roots(*move(factors[0], target))[None]
 
 
 def solution(mesh):

time: 57.1 us -> 50.7 us (0.89)
  Pallas kernels: 55.6 us -> 49.1 us
    pallas_call x2, Pallas kernels: 55.6 us -> 49.1 us  [the longest x1 39.1 us: move(): pl.pallas_call(move_kernel, out_shape=(jax.ShapeDtypeStruct((CAP - 1, DEV...]
where the time goes in v3:
time: 50.7 us; the launch traced here: 50.5 us
  Pallas kernels  49.1 us (97%)
  local copies, waits for them, and re-layouts  1.3 us (3%)
    pallas_call x1, Pallas kernels, move(): pl.pallas_call(move_kernel, out_shape=(jax.ShapeDtypeStruct((CAP - 1, DEV...  39.1 us
    pallas_call x1, Pallas kernels, roots(): pl.pallas_call(root_kernel, out_shape=jax.ShapeDtypeStruct((CAP, 512, 512...  10 us
    unnamed x1, local copies, waits for them, and re-layouts  1.3 us

profile of v3, /device:TPU:1, one launch (start us, length us, event | category | flops | bytes accessed | tf_op | source)
XLA Modules:
  0.0 50.5 jit_solution(1502939603831832260)
XLA Ops:
  0.0 1.3 %copy.3.t_ref = s32[2,1]{1,0:T(2,128)} copy(s32[2,1]{0,1:T(1,128)} %param.3) | data formatting | bytes 16 | tf_op args[1]
  1.3 39.1 %move.1 = (bf16[2,128,8,128]{3,2,1,0:T(8,128)(2,1)}, f32[16,128]{1,0:T(8,128)}, f32[512,512]{1,0:T(8,128)}) custom-call(bf16[2,512,512]{2,1,0:T(8,128)(2,1)} %bitcast.2, s32[2,1]{1,0:T(2,128)} %copy.3.t_ref), custom_call_target="tpu_custom_call" | custom-call | tf_op jit(solution)/shard_map/move/pallas_call | solution.py:272
  40.4 10.0 %roots.1 = f32[3,512,512]{2,1,0:T(8,128)} custom-call(bf16[2,128,8,128]{3,2,1,0:T(8,128)(2,1)} %get-tuple-element.8.g_ref, f32[16,128]{1,0:T(8,128)} %get-tuple-element.9.aux_ref, f32[512,512]{1,0:T(8,128)} %get-tuple-element.10.first_any), custom_call_target="tpu_custom_call" | custom-call | tf_op jit(solution)/shard_map/roots/pallas_call | solution.py:325

commit v4 on v3

--- a/solution.py
+++ b/solution.py
@@ -13,6 +13,7 @@
 DEVICES = 128
 HALF = 256
 CAP = 3
+GRANT = 32 << 20
 F32 = jnp.float32
 BF16 = jnp.bfloat16
 
@@ -67,7 +68,7 @@
                 send1[h, start : start + 32] = piece.reshape(32, 8, 128)
     lane = iota((1, 128), 1)
     facts = jnp.where(lane == 0, t_ref[0:1, 0:1].astype(F32), 0.0)
-    facts = jnp.where(lane == 1, t_ref[1:2, 0:1].astype(F32), facts)
+    facts = jnp.where(lane == 1, t_ref[0:1, 1:2].astype(F32), facts)
     facts_ref[...] = jnp.where(lane == 2, sq, facts)
 
 
@@ -198,21 +199,26 @@
 
 
 def move_kernel(
-    f_any, t_ref, g_ref, aux_ref, out_any,
-    f_ref, send1, got1, facts, all_facts, diagonal, all_diagonal, send2, got2, order, order_s,
+    f_hbm, t_hbm, g_any, aux_ref, out_any,
+    t_ref, f_ref, send1, got1, facts, all_facts, diagonal, all_diagonal, send2, got2, order, order_s,
     root, block, x, y, z,
-    facts_out, facts_in, diagonal_out, diagonal_in, out1, in1, out2, in2, local,
+    facts_out, facts_in, diagonal_out, diagonal_in, out1, in1, out2, in2, local, stored,
 ):
     here = tuple(lax.axis_index(a) for a in AXES)
     me = ((here[0] * 2 + here[1]) * 4 + here[2]) * 4 + here[3]
-    load = pltpu.make_async_copy(f_any, f_ref, local)
-    load.start()
+    loads = [
+        pltpu.make_async_copy(f_hbm, f_ref, stored.at[0]),
+        pltpu.make_async_copy(t_hbm, t_ref, stored.at[1]),
+    ]
+    for load in loads:
+        load.start()
     barrier = pltpu.get_barrier_semaphore()
     each_peer(
         here,
         lambda there, _: pl.semaphore_signal(barrier, 1, device_id=there, device_id_type=MESH),
     )
-    load.wait()
+    for load in loads:
+        load.wait()
     pack(f_ref, t_ref, send1, facts, diagonal)
     pl.semaphore_wait(barrier, DEVICES - 1)
 
@@ -257,14 +263,20 @@
     for s in range(CAP):
         aux_ref[2 * s : 2 * s + 2, :] = all_diagonal[place(order_s[s, me])].astype(F32)
     settle(got2.at[0, 0 : DEVICES - 1], in2.at[0], out2.at[0])
-    for _ in begin(0, got2.at[0], aux_ref, root, block, x, y, z):
-        pass
-    done = pltpu.make_async_copy(root, out_any, local)
-    done.start()
-    for s in range(1, CAP):
+    stores = [pltpu.make_async_copy(root, out_any, stored.at[0])]
+    stores += [pltpu.make_async_copy(got2.at[s], g_any.at[s - 1], stored.at[s]) for s in range(1, CAP)]
+
+    def store(s):
         settle(got2.at[s, 0 : DEVICES - 1], in2.at[s], out2.at[s])
-        g_ref[s - 1] = got2[s]
-    done.wait()
+        stores[s].start()
+
+    for step, _ in enumerate(begin(0, got2.at[0], aux_ref, root, block, x, y, z)):
+        if step == 4:
+            store(1)
+    stores[0].start()
+    store(2)
+    for copy in stores:
+        copy.wait()
 
 
 def move(factors, target):
@@ -276,9 +288,10 @@
             jax.ShapeDtypeStruct((16, 128), F32),
             jax.ShapeDtypeStruct((512, 512), F32),
         ),
-        in_specs=[pl.BlockSpec(memory_space=pl.ANY), pl.BlockSpec(memory_space=vmem)],
-        out_specs=[pl.BlockSpec(memory_space=vmem)] * 2 + [pl.BlockSpec(memory_space=pl.ANY)],
+        in_specs=[pl.BlockSpec(memory_space=pltpu.HBM)] * 2,
+        out_specs=[pl.BlockSpec(memory_space=m) for m in (pl.ANY, vmem, pl.ANY)],
         scratch_shapes=[
+            vmem((1, 2), jnp.int32),
             vmem((2, 512, 512), BF16),
             vmem((2, DEVICES, 8, 128), BF16),
             vmem((2, DEVICES, 8, 128), BF16),
@@ -295,27 +308,26 @@
             vmem((2, 512, 512), BF16),
             vmem((2, 512, 512), BF16),
             vmem((2, 512, 512), BF16),
-            dma, dma, dma, dma, dma, dma, dma((CAP,)), dma((CAP,)), dma,
+            dma, dma, dma, dma, dma, dma, dma((CAP,)), dma((CAP,)), dma, dma((CAP,)),
         ],
-        compiler_params=pltpu.CompilerParams(collective_id=0, has_side_effects=True),
+        compiler_params=pltpu.CompilerParams(collective_id=0, has_side_effects=True, vmem_limit_bytes=GRANT),
         name="move",
     )(factors, target)
 
 
-def root_kernel(g_ref, aux_ref, first_any, out_any, root, block, x, y, z, sems):
-    load = pltpu.make_async_copy(first_any, root.at[0], sems.at[0])
-    load.start()
-    works = [
-        begin(s, g_ref.at[s - 1], aux_ref, root.at[s], *(r.at[s - 1] for r in (block, x, y, z)))
-        for s in range(1, CAP)
-    ]
-    copies = [pltpu.make_async_copy(root.at[s], out_any.at[s], sems.at[s]) for s in range(CAP)]
-    for step, _ in enumerate(itertools.zip_longest(*works)):
-        if step == 3:
-            load.wait()
-            copies[0].start()
-    for copy in copies[1:]:
-        copy.start()
+def root_kernel(g_ref, aux_ref, first_ref, out_any, root, block, x, y, z, sems):
+    copies = [pltpu.make_async_copy(first_ref, out_any.at[0], sems.at[0])]
+    copies[0].start()
+    works = []
+    for s in range(1, CAP):
+        places = (r.at[s - 1] for r in (root, block, x, y, z))
+        works.append(begin(s, g_ref.at[s - 1], aux_ref, *places))
+        copies.append(pltpu.make_async_copy(root.at[s - 1], out_any.at[s], sems.at[s]))
+    for step in range(7):
+        for s, work in enumerate(works):
+            next(work, None)
+            if step == 6:
+                copies[s + 1].start()
     for copy in copies:
         copy.wait()
 
@@ -325,26 +337,23 @@
     return pl.pallas_call(
         root_kernel,
         out_shape=jax.ShapeDtypeStruct((CAP, 512, 512), F32),
-        in_specs=[
-            pl.BlockSpec(memory_space=vmem),
-            pl.BlockSpec(memory_space=vmem),
-            pl.BlockSpec(memory_space=pl.ANY),
-        ],
+        in_specs=[pl.BlockSpec(memory_space=vmem)] * 3,
         out_specs=pl.BlockSpec(memory_space=pl.ANY),
         scratch_shapes=[
-            vmem((CAP, 512, 512), F32),
+            vmem((CAP - 1, 512, 512), F32),
             vmem((CAP - 1, 512, 512), BF16),
             vmem((CAP - 1, 2, 512, 512), BF16),
             vmem((CAP - 1, 2, 512, 512), BF16),
             vmem((CAP - 1, 2, 512, 512), BF16),
             pltpu.SemaphoreType.DMA((CAP,)),
         ],
+        compiler_params=pltpu.CompilerParams(vmem_limit_bytes=GRANT),
         name="roots",
     )(moved, aux, first)
 
 
 def shards(factors, target):
-    return roots(*move(factors[0], target))[None]
+    return roots(*move(pltpu.with_memory_space_constraint(factors[0], pltpu.HBM), pltpu.with_memory_space_constraint(target.T, pltpu.HBM)))[None]
 
 
 def solution(mesh):

time: 50.7 us -> 46.1 us (0.909)
  Pallas kernels: 49.1 us -> 45.8 us
  local copies, waits for them, and re-layouts: 1.3 us -> 0 us
    pallas_call x1, Pallas kernels: 39.1 us -> 37.3 us  [move(): pl.pallas_call(move_kernel, out_shape=(jax.ShapeDtypeStruct((CAP - 1, DEV...]
    pallas_call x1, Pallas kernels: 10 us -> 8.49 us  [roots(): pl.pallas_call(root_kernel, out_shape=jax.ShapeDtypeStruct((CAP, 512, 512...]
    unnamed x1 -> x0, local copies, waits for them, and re-layouts: 1.3 us -> none
where the time goes in v4:
time: 46.1 us; the launch traced here: 46 us
  Pallas kernels  45.8 us (99%)
    pallas_call x1, Pallas kernels, move(): pl.pallas_call(move_kernel, out_shape=(jax.ShapeDtypeStruct((CAP - 1, DEV...  37.3 us
    pallas_call x1, Pallas kernels, roots(): pl.pallas_call(root_kernel, out_shape=jax.ShapeDtypeStruct((CAP, 512, 512...  8.49 us

profile of v4, /device:TPU:1, one launch (start us, length us, event | category | flops | bytes accessed | tf_op | source)
XLA Modules:
  0.0 46.0 jit_solution(13947304032265179055)
XLA Ops:
  0.0 37.3 %move.1 = (bf16[2,128,8,128]{3,2,1,0:T(8,128)(2,1)S(1)}, f32[16,128]{1,0:T(8,128)S(1)}, f32[512,512]{1,0:T(8,128)S(1)}) custom-call(bf16[2,512,512]{2,1,0:T(8,128)(2,1)} %bitcast.3, s32[1,2]{1,0:T(1,128)} %bitcast.4), custom_call_target="tpu_custom_call" | custom-call | tf_op jit(solution)/shard_map/move/pallas_call | solution.py:284
  37.3 8.5 %roots.1 = f32[3,512,512]{2,1,0:T(8,128)} custom-call(bf16[2,128,8,128]{3,2,1,0:T(8,128)(2,1)S(1)} %get-tuple-element.8.g_ref, f32[16,128]{1,0:T(8,128)S(1)} %get-tuple-element.9.aux_ref, f32[512,512]{1,0:T(8,128)S(1)} %get-tuple-element.10.first_ref), custom_call_target="tpu_custom_call" | custom-call | tf_op jit(solution)/shard_map/roots/pallas_call | solution.py:337

commit v5 on v4

--- a/solution.py
+++ b/solution.py
@@ -26,24 +26,25 @@
     return jnp.sum(jnp.sum(value, axis=1, keepdims=True), axis=0, keepdims=True)
 
 
+def step_of(digit):
+    return (0x36 >> (2 * (digit & 3))) & 3
+
+
 def peer(k, here):
     y, c, z, x = here
-    k = (k * 37) & (DEVICES - 1)
     there = (
-        (y + ((k >> 4) & 3)) & 3,
-        (c + (k >> 6)) & 1,
-        (z + ((k >> 2) & 3)) & 3,
-        (x + (k & 3)) & 3,
+        (y + step_of(k >> 4)) & 3,
+        (c + 1 - (k >> 6)) & 1,
+        (z + step_of(k >> 2)) & 3,
+        (x + step_of(k)) & 3,
     )
     return there, ((there[0] * 2 + there[1]) * 4 + there[2]) * 4 + there[3]
 
 
 def each_peer(here, do):
-    for start, stop, unroll in ((1, 8, 7), (8, DEVICES, 8)):
-
-        @pl.loop(start, stop, unroll=unroll)
-        def _(k):
-            do(*peer(k, here))
+    @pl.loop(0, DEVICES - 1, unroll=DEVICES - 1)
+    def _(k):
+        do(*peer(k, here))
 
 
 def pack(f_ref, t_ref, send1, facts_ref, diagonal_ref):
@@ -53,10 +54,9 @@
     for h in range(2):
         a = f_ref[h, 0:HALF, 0:HALF].astype(F32)
         b = f_ref[h, 0:HALF, HALF:]
-        c = f_ref[h, HALF:, 0:HALF].astype(F32)
         d = f_ref[h, HALF:, HALF:].astype(F32)
         bf = b.astype(F32)
-        sq = sq + total(a * a + bf * bf + c * c + d * d)
+        sq = sq + total(a * a + 2.0 * (bf * bf) + d * d)
         v = jnp.where(row <= col, a, d).astype(BF16)
         diagonal = jnp.sum(jnp.where(row == col, d, 0.0), axis=0, keepdims=True)
         diagonal = jnp.where(line == 0, diagonal[:, 0:128], diagonal[:, 128:])
@@ -134,6 +134,13 @@
     return product((a[0], b[0]), (a[0], b[1]), (a[1], b[0]))
 
 
+def squared(a):
+    high = product((a.at[0], a.at[0]))
+    cross = dot(a[0], a[1])
+    sides = ((LEFT, LEFT), (LEFT, RIGHT), (RIGHT, RIGHT))
+    return [t + (cross[r, c] + cross[c, r].T) for t, (r, c) in zip(high, sides)]
+
+
 def keep(ref, value):
     places = (LEFT, LEFT), (LEFT, RIGHT), (RIGHT, RIGHT), (RIGHT, LEFT)
     for (r, c), tile in zip(places, (*value, value[1].T)):
@@ -171,21 +178,21 @@
     square = product((block, block))
     keep(x, [1.25 * e - (2.5 * q) * a + (s * q) * q for e, a, s in zip(eyes, tiles(block), square)])
     yield
-    keep(y, [t * q for t in product((x.at[0], block), (x.at[1], block))])
-    yield
-    step = [e - t for e, t in zip(eyes, times(x, y))]
+    keep(y, squared(x))
+    yield
+    step = [e - t * q for e, t in zip(eyes, product((y.at[0], block), (y.at[1], block)))]
     keep(z, step)
     yield
-    square = times(z, z)
+    square = squared(z)
     keep(x, square)
     keep(y, [1.25 * t - s for t, s in zip(step, square)])
     yield
-    keep(z, times(x, y))
-    yield
-    both = [1.25 * t - f for t, f in zip(step, times(x, z))]
-    keep(y, both)
-    yield
-    rest = product((y.at[0], block), (y.at[1], block))
+    keep(z, squared(x))
+    yield
+    both = [1.25 * t - f for t, f in zip(step, times(z, y))]
+    keep(x, both)
+    yield
+    rest = product((x.at[0], block), (x.at[1], block))
     root = [(1.25 * t - r * q) * factor for t, r in zip(both, rest)]
     out[LEFT, LEFT] = root[0]
     out[LEFT, RIGHT] = root[1]

time: 46.1 us -> 41.5 us (0.900)
  Pallas kernels: 45.8 us -> 40.7 us
    pallas_call x1, Pallas kernels: 37.3 us -> 33 us  [move(): pl.pallas_call(move_kernel, out_shape=(jax.ShapeDtypeStruct((CAP - 1, DEV...]
    pallas_call x1, Pallas kernels: 8.49 us -> 7.68 us  [roots(): pl.pallas_call(root_kernel, out_shape=jax.ShapeDtypeStruct((CAP, 512, 512...]
where the time goes in v5:
time: 41.5 us; the launch traced here: 40.9 us
  Pallas kernels  40.7 us (98%)
    pallas_call x1, Pallas kernels, move(): pl.pallas_call(move_kernel, out_shape=(jax.ShapeDtypeStruct((CAP - 1, DEV...  33 us
    pallas_call x1, Pallas kernels, roots(): pl.pallas_call(root_kernel, out_shape=jax.ShapeDtypeStruct((CAP, 512, 512...  7.68 us

profile of v5, /device:TPU:1, one launch (start us, length us, event | category | flops | bytes accessed | tf_op | source)
XLA Modules:
  0.0 40.9 jit_solution(12659586767151465950)
XLA Ops:
  0.0 33.0 %move.1 = (bf16[2,128,8,128]{3,2,1,0:T(8,128)(2,1)S(1)}, f32[16,128]{1,0:T(8,128)S(1)}, f32[512,512]{1,0:T(8,128)S(1)}) custom-call(bf16[2,512,512]{2,1,0:T(8,128)(2,1)} %bitcast.3, s32[1,2]{1,0:T(1,128)} %bitcast.4), custom_call_target="tpu_custom_call" | custom-call | tf_op jit(solution)/shard_map/move/pallas_call | solution.py:291
  33.1 7.7 %roots.1 = f32[3,512,512]{2,1,0:T(8,128)} custom-call(bf16[2,128,8,128]{3,2,1,0:T(8,128)(2,1)S(1)} %get-tuple-element.8.g_ref, f32[16,128]{1,0:T(8,128)S(1)} %get-tuple-element.9.aux_ref, f32[512,512]{1,0:T(8,128)S(1)} %get-tuple-element.10.first_ref), custom_call_target="tpu_custom_call" | custom-call | tf_op jit(solution)/shard_map/roots/pallas_call | solution.py:344

commit v6 on v5

--- a/solution.py
+++ b/solution.py
@@ -206,16 +206,16 @@
 
 
 def move_kernel(
-    f_hbm, t_hbm, g_any, aux_ref, out_any,
+    f_hbm, t_hbm, g_ref, aux_ref, first_ref,
     t_ref, f_ref, send1, got1, facts, all_facts, diagonal, all_diagonal, send2, got2, order, order_s,
-    root, block, x, y, z,
-    facts_out, facts_in, diagonal_out, diagonal_in, out1, in1, out2, in2, local, stored,
+    block, x, y, z,
+    facts_out, facts_in, diagonal_out, diagonal_in, out1, in1, out2, in2, local, loaded,
 ):
     here = tuple(lax.axis_index(a) for a in AXES)
     me = ((here[0] * 2 + here[1]) * 4 + here[2]) * 4 + here[3]
     loads = [
-        pltpu.make_async_copy(f_hbm, f_ref, stored.at[0]),
-        pltpu.make_async_copy(t_hbm, t_ref, stored.at[1]),
+        pltpu.make_async_copy(f_hbm, f_ref, loaded.at[0]),
+        pltpu.make_async_copy(t_hbm, t_ref, loaded.at[1]),
     ]
     for load in loads:
         load.start()
@@ -260,7 +260,7 @@
 
     for s in range(CAP):
 
-        @pl.loop(0, DEVICES, unroll=8)
+        @pl.loop(0, DEVICES, unroll=32)
         def _(d, s=s):
             send2[s, d] = got1[place(order_s[s, d])]
 
@@ -270,20 +270,15 @@
     for s in range(CAP):
         aux_ref[2 * s : 2 * s + 2, :] = all_diagonal[place(order_s[s, me])].astype(F32)
     settle(got2.at[0, 0 : DEVICES - 1], in2.at[0], out2.at[0])
-    stores = [pltpu.make_async_copy(root, out_any, stored.at[0])]
-    stores += [pltpu.make_async_copy(got2.at[s], g_any.at[s - 1], stored.at[s]) for s in range(1, CAP)]
 
     def store(s):
         settle(got2.at[s, 0 : DEVICES - 1], in2.at[s], out2.at[s])
-        stores[s].start()
-
-    for step, _ in enumerate(begin(0, got2.at[0], aux_ref, root, block, x, y, z)):
-        if step == 4:
+        g_ref[s - 1] = got2[s]
+
+    for step, _ in enumerate(begin(0, got2.at[0], aux_ref, first_ref, block, x, y, z)):
+        if step == 5:
             store(1)
-    stores[0].start()
     store(2)
-    for copy in stores:
-        copy.wait()
 
 
 def move(factors, target):
@@ -296,7 +291,7 @@
             jax.ShapeDtypeStruct((512, 512), F32),
         ),
         in_specs=[pl.BlockSpec(memory_space=pltpu.HBM)] * 2,
-        out_specs=[pl.BlockSpec(memory_space=m) for m in (pl.ANY, vmem, pl.ANY)],
+        out_specs=[pl.BlockSpec(memory_space=vmem)] * 3,
         scratch_shapes=[
             vmem((1, 2), jnp.int32),
             vmem((2, 512, 512), BF16),
@@ -310,12 +305,11 @@
             vmem((CAP, DEVICES, 8, 128), BF16),
             vmem((8, 128), jnp.int32),
             pltpu.SMEM((8, 128), jnp.int32),
-            vmem((512, 512), F32),
             vmem((512, 512), BF16),
             vmem((2, 512, 512), BF16),
             vmem((2, 512, 512), BF16),
             vmem((2, 512, 512), BF16),
-            dma, dma, dma, dma, dma, dma, dma((CAP,)), dma((CAP,)), dma, dma((CAP,)),
+            dma, dma, dma, dma, dma, dma, dma((CAP,)), dma((CAP,)), dma, dma((2,)),
         ],
         compiler_params=pltpu.CompilerParams(collective_id=0, has_side_effects=True, vmem_limit_bytes=GRANT),
         name="move",

time: 41.5 us -> 40.9 us (0.986)
  no operation moved by 1% of the time
where the time goes in v6:
time: 40.9 us; the launch traced here: 40.6 us
  Pallas kernels  40.4 us (99%)
    pallas_call x1, Pallas kernels, move(): pl.pallas_call(move_kernel, out_shape=(jax.ShapeDtypeStruct((CAP - 1, DEV...  32.7 us
    pallas_call x1, Pallas kernels, roots(): pl.pallas_call(root_kernel, out_shape=jax.ShapeDtypeStruct((CAP, 512, 512...  7.68 us

profile of v6, /device:TPU:1, one launch (start us, length us, event | category | flops | bytes accessed | tf_op | source)
XLA Modules:
  0.0 40.6 jit_solution(14823347971483007014)
XLA Ops:
  0.0 32.7 %move.1 = (bf16[2,128,8,128]{3,2,1,0:T(8,128)(2,1)S(1)}, f32[16,128]{1,0:T(8,128)S(1)}, f32[512,512]{1,0:T(8,128)S(1)}) custom-call(bf16[2,512,512]{2,1,0:T(8,128)(2,1)} %bitcast.3, s32[1,2]{1,0:T(1,128)} %bitcast.4), custom_call_target="tpu_custom_call" | custom-call | tf_op jit(solution)/shard_map/move/pallas_call | solution.py:286
  32.7 7.7 %roots.1 = f32[3,512,512]{2,1,0:T(8,128)} custom-call(bf16[2,128,8,128]{3,2,1,0:T(8,128)(2,1)S(1)} %get-tuple-element.8.g_ref, f32[16,128]{1,0:T(8,128)S(1)} %get-tuple-element.9.aux_ref, f32[512,512]{1,0:T(8,128)S(1)} %get-tuple-element.10.first_ref), custom_call_target="tpu_custom_call" | custom-call | tf_op jit(solution)/shard_map/roots/pallas_call | solution.py:338

commit v7 on v6

--- a/solution.py
+++ b/solution.py
@@ -41,8 +41,8 @@
     return there, ((there[0] * 2 + there[1]) * 4 + there[2]) * 4 + there[3]
 
 
-def each_peer(here, do):
-    @pl.loop(0, DEVICES - 1, unroll=DEVICES - 1)
+def each_peer(here, do, start=0, stop=DEVICES - 1):
+    @pl.loop(start, stop, unroll=stop - start)
     def _(k):
         do(*peer(k, here))
 
@@ -229,14 +229,14 @@
     pack(f_ref, t_ref, send1, facts, diagonal)
     pl.semaphore_wait(barrier, DEVICES - 1)
 
-    def send(source, target, gone, came):
+    def send(source, target, gone, came, *part):
         def start(there, index):
             pltpu.make_async_remote_copy(
                 src_ref=source(index), dst_ref=target, send_sem=gone, recv_sem=came,
                 device_id=there, device_id_type=MESH,
             ).start()
 
-        each_peer(here, start)
+        each_peer(here, start, *part)
 
     def settle(buffer, *sems):
         for sem in sems:
@@ -260,12 +260,14 @@
 
     for s in range(CAP):
 
-        @pl.loop(0, DEVICES, unroll=32)
-        def _(d, s=s):
-            send2[s, d] = got1[place(order_s[s, d])]
-
-        send(lambda index, s=s: send2.at[s, index], got2.at[s, me], out2.at[s], in2.at[s])
-        got2[s, me] = send2[s, me]
+        def gather(_, index, s=s):
+            send2[s, index] = got1[place(order_s[s, index])]
+
+        bounds = (0, 32, 64, 96, DEVICES - 1) if s == 0 else (0, DEVICES - 1)
+        for part in zip(bounds, bounds[1:]):
+            each_peer(here, gather, *part)
+            send(lambda index, s=s: send2.at[s, index], got2.at[s, me], out2.at[s], in2.at[s], *part)
+        got2[s, me] = got1[place(order_s[s, me])]
     settle(all_diagonal.at[:, 0 : DEVICES - 1], diagonal_in, diagonal_out)
     for s in range(CAP):
         aux_ref[2 * s : 2 * s + 2, :] = all_diagonal[place(order_s[s, me])].astype(F32)

time: 40.9 us -> 40.9 us (level)
  no operation moved by 1% of the time
where the time goes in v7:
time: 40.9 us; the launch traced here: 40.7 us
  Pallas kernels  40.5 us (99%)
    pallas_call x1, Pallas kernels, move(): pl.pallas_call(move_kernel, out_shape=(jax.ShapeDtypeStruct((CAP - 1, DEV...  32.8 us
    pallas_call x1, Pallas kernels, roots(): pl.pallas_call(root_kernel, out_shape=jax.ShapeDtypeStruct((CAP, 512, 512...  7.68 us

profile of v7, /device:TPU:1, one launch (start us, length us, event | category | flops | bytes accessed | tf_op | source)
XLA Modules:
  0.0 40.7 jit_solution(4160537775717213169)
XLA Ops:
  0.0 32.8 %move.1 = (bf16[2,128,8,128]{3,2,1,0:T(8,128)(2,1)S(1)}, f32[16,128]{1,0:T(8,128)S(1)}, f32[512,512]{1,0:T(8,128)S(1)}) custom-call(bf16[2,512,512]{2,1,0:T(8,128)(2,1)} %bitcast.3, s32[1,2]{1,0:T(1,128)} %bitcast.4), custom_call_target="tpu_custom_call" | custom-call | tf_op jit(solution)/shard_map/move/pallas_call | solution.py:288
  32.8 7.7 %roots.1 = f32[3,512,512]{2,1,0:T(8,128)} custom-call(bf16[2,128,8,128]{3,2,1,0:T(8,128)(2,1)S(1)} %get-tuple-element.8.g_ref, f32[16,128]{1,0:T(8,128)S(1)} %get-tuple-element.9.aux_ref, f32[512,512]{1,0:T(8,128)S(1)} %get-tuple-element.10.first_ref), custom_call_target="tpu_custom_call" | custom-call | tf_op jit(solution)/shard_map/roots/pallas_call | solution.py:340
